TPU v7x, 32 devices: a whole 2x2x4 slice. The times are simulated.
32 devices in a mesh: section: 4 (over y, core), replica: 8 (over z, x).
Axes of the slice: x: 2, y: 2, z: 4, core: 2. Of those that a mesh axis runs over, the one named last changes fastest.
Arguments:
- gradient: bfloat16 [512, 32768], P('section', 'replica'), may hold values from -1300 to 1300
- residual: float32 [512, 32768], P('section', 'replica'), may hold values from -6 to 6
- block_ids: int32 [4, 64], P('section', 'replica'), may hold values from 0 to 15, as said below
- block_counts: int32 [4, 8], P('section', 'replica'), may hold values from 1 to 8, as said below
Outputs:
- new_residual: float32 [512, 32768], P('section', 'replica')
- update: bfloat16 [512, 4096], P('section', 'replica')
Inputs may be any that keep to these rules, and one draw needn't show every extreme that they name: `block_ids`: each device's 8 block numbers are distinct; only the first block_counts of them are selected. `block_counts`: in every section some replica selects exactly 8 blocks; the others select at most 4.
All inputs are finite; a program needn't handle non-finite values.
Results may differ from a plain program's by a relative error of at most 0.013.
Values may be sent and summed in bfloat16 or wider, within the bound.
A program may use at most 64 MiB of HBM per device.

v0:
```python
import jax
import jax.numpy as jnp
from jax import lax
from jax.sharding import PartitionSpec as P

BLK = 8


scale_level = 1.0
epsilon = 1e-06


def deposit(packed, owners, block_total):
    one_hot = (owners[:, None] == jnp.arange(block_total, dtype=jnp.int32)[None, :]).astype(
        jnp.bfloat16
    )
    return jnp.einsum("kb,kxc->bxc", one_hot, packed, preferred_element_type=jnp.float32)


def per_device(gradient, residual, block_ids, block_counts):
    row_count, width = gradient.shape
    replicas = lax.axis_size("replica")
    col_count = width // replicas
    block_total = row_count // BLK
    slot_count = block_ids.shape[1]
    accumulated = gradient.astype(jnp.float32) + residual
    slot_ids = block_ids[0]
    live_slot = jnp.arange(slot_count, dtype=jnp.int32) < block_counts[0, 0]
    hit_table = (
        slot_ids[:, None] == jnp.arange(block_total, dtype=jnp.int32)[None, :]
    ) & live_slot[:, None]
    chosen = jnp.any(hit_table, axis=0)
    row_chosen = jnp.repeat(chosen, BLK)[:, None]
    sent = jnp.where(
        row_chosen, accumulated.astype(jnp.bfloat16).astype(jnp.float32), jnp.float32(0.0)
    )
    new_residual = accumulated - sent
    picked = accumulated.reshape(block_total, BLK, width)[slot_ids]
    packed_blocks = jnp.where(live_slot[:, None, None], picked, jnp.float32(0.0)).astype(
        jnp.bfloat16
    )
    column_parts = packed_blocks.reshape(slot_count, BLK, replicas, col_count)
    received = lax.all_to_all(column_parts, "replica", split_axis=2, concat_axis=0, tiled=True)
    owners = lax.all_gather(slot_ids, "replica", axis=0, tiled=True)
    flat_received = received.reshape(replicas * slot_count, BLK, col_count)
    summed = deposit(flat_received, owners, block_total).reshape(row_count, col_count)
    local_square = jnp.sum(summed * summed)
    norm_total = lax.psum(local_square, ("section", "replica"))
    element_count = lax.axis_size("section") * row_count * width
    root_mean = jnp.sqrt(norm_total / element_count + epsilon)
    clip_factor = scale_level / root_mean
    update = (summed * clip_factor).astype(jnp.bfloat16)
    return (new_residual, update)


def solution(mesh):
    in_specs = (
        P("section", "replica"),
        P("section", "replica"),
        P("section", "replica"),
        P("section", "replica"),
    )
    out_specs = (P("section", "replica"), P("section", "replica"))
    return jax.shard_map(
        per_device, mesh=mesh, in_specs=in_specs, out_specs=out_specs, check_vma=False
    )
```

profile of v0, /device:TPU:0, one launch (start us, length us, event | category | flops | bytes accessed | tf_op | source)
XLA Modules:
  0.0 75.5 jit_solution(17205072803402985142)
XLA Ops:
  1.3 0.7 fusion.10
  2.0 3.0 %fusion.1 = bf16[16,8,4096]{2,1,0:T(8,128)(2,1)} fusion(f32[128,4096]{1,0:T(8,128)} %param.5, bf16[128,4096]{1,0:T(8,128)(2,1)} %param.4), kind=kLoop, calls=%fused_computation.5 | loop fusion | flops 1572864 | bytes 4194304 | tf_op jit(solution)/shard_map/reshape | solution.py:38
  5.0 0.0 copy-start.2
  5.0 0.0 copy-start.3
  5.0 0.0 copy-start
  5.0 0.0 copy-start.1
  5.0 2.7 %gather_fusion = bf16[8,8,4096]{2,1,0:T(8,128)(2,1)} fusion(bf16[16,8,4096]{2,1,0:T(8,128)(2,1)} %fusion.1, s32[1024]{0:T(1024)S(1)} %pad_clamp_fusion), kind=kCustom, calls=%fused_computation | custom fusion | bytes 1048608 | tf_op jit(solution)/shard_map/gather | solution.py:38
  7.8 1.3 %fusion = bf16[8,8,8,512]{3,2,1,0:T(8,128)(2,1)S(1)} fusion(bf16[8,8,8,512]{3,1,2,0:T(8,128)(2,1)} %bitcast.34, pred[8]{0:T(512)(128)(4,1)S(1)} %iota_compare_fusion.2), kind=kLoop, calls=%fused_computation.4 | loop fusion | flops 262144 | bytes 1048584 | tf_op jit(solution)/shard_map/convert_element_type | solution.py:39
  9.0 1.0 %copy.11 = bf16[8,8,8,512]{3,1,0,2:T(8,128)(2,1)} copy(bf16[8,8,8,512]{3,2,1,0:T(8,128)(2,1)S(1)} %fusion) | data formatting | bytes 1048576 | tf_op jit(solution)/shard_map/convert_element_type | solution.py:39
  10.0 7.3 %all-to-all-start = ((bf16[8,8,8,512]{3,1,0,2:T(8,128)(2,1)}), bf16[8,8,8,512]{3,1,0,2:T(8,128)(2,1)}, u32[]{:S(2)}, u32[]{:S(2)}) async-start(bf16[8,8,8,512]{3,1,0,2:T(8,128)(2,1)} %copy.11), calls=%async_computation | async-start | bytes 1048576 | tf_op jit(solution)/shard_map/all_to_all | solution.py:43
  17.3 0.0 copy-done.2
  17.3 0.1 fusion.9
  17.4 0.0 copy-done.3
  17.4 0.6 dynamic-slice
  18.6 0.1 bitcast_dynamic-update-slice_fusion
  18.7 13.5 %all-reduce = s32[64]{0:T(128)S(1)} all-reduce(s32[64]{0:T(128)S(1)} %bitcast_dynamic-update-slice_fusion), channel_id=2, replica_groups=mesh['section'=4,'replica'=8] {'replica'}, use_global_device_ids=true, to_apply=%add | all-reduce | flops 64 | bytes 512
  32.2 0.1 broadcast_in_dim.35
  32.3 0.1 broadcast_in_dim.36
  32.4 0.0 copy-done
  32.4 0.0 copy-done.1
  32.4 1.7 %select_subtract_fusion = f32[128,4096]{1,0:T(8,128)} fusion(f32[128,4096]{1,0:T(8,128)S(1)} %copy-done, bf16[128,4096]{1,0:T(8,128)(2,1)S(1)} %copy-done.1, pred[128]{0:T(512)(128)(4,1)S(1)} %broadcast_in_dim.36), kind=kLoop, calls=%fused_computation.1 | loop fusion | flops 3145728 | bytes 5243008 | tf_op jit(solution)/shard_map/sub | solution.py:37
  34.0 0.0 all-to-all-done
  34.0 1.9 %multiply_reduce_fusion = (f32[]{:T(128)}, f32[16,8,512]{2,0,1:T(8,128)S(1)}) fusion(bf16[8,8,8,1,512]{4,2,1,0,3:T(8,128)(2,1)} %bitcast.8, s32[64]{0:T(128)S(1)} %all-reduce), kind=kOutput, calls=%fused_computation.10 | convolution fusion | flops 8520703 | bytes 786692 | tf_op jit(solution)/shard_map/kb,kxc->bxc/dot_general | solution.py:17
  36.0 38.0 %psum.7 = f32[]{:T(128)} all-reduce(f32[]{:T(128)} %get-tuple-element.2), channel_id=1, replica_groups=mesh['section'=4,'replica'=8] {'section','replica'}, use_global_device_ids=true, to_apply=%region_2.3 | all-reduce | flops 1 | bytes 8 | tf_op jit(solution)/shard_map/psum | solution.py:48
  74.7 0.7 copy.23
  (4 shorter events, 0.0 us)
Async XLA Ops:
  5.0 12.3 %copy-start.2 = (s32[1,8]{1,0:T(1,128)S(1)}, s32[1,8]{1,0:T(1,128)}, u32[]{:S(2)}) copy-start(s32[1,8]{1,0:T(1,128)} %param.6) | copy-start | bytes 100
  5.0 12.4 %copy-start.3 = (u32[32]{0:T(128)S(1)}, u32[32]{0:T(128)}, u32[]{:S(2)}) copy-start(u32[32]{0:T(128)} %constant.18) | copy-start | bytes 388
  5.0 27.4 %copy-start = (f32[128,4096]{1,0:T(8,128)S(1)}, f32[128,4096]{1,0:T(8,128)}, u32[]{:S(2)}) copy-start(f32[128,4096]{1,0:T(8,128)} %param.5) | copy-start | bytes 6291460
  5.0 27.4 %copy-start.1 = (bf16[128,4096]{1,0:T(8,128)(2,1)S(1)}, bf16[128,4096]{1,0:T(8,128)(2,1)}, u32[]{:S(2)}) copy-start(bf16[128,4096]{1,0:T(8,128)(2,1)} %param.4) | copy-start | bytes 3145732
  10.0 24.1 %all-to-all-start = ((bf16[8,8,8,512]{3,1,0,2:T(8,128)(2,1)}), bf16[8,8,8,512]{3,1,0,2:T(8,128)(2,1)}, u32[]{:S(2)}, u32[]{:S(2)}) async-start(bf16[8,8,8,512]{3,1,0,2:T(8,128)(2,1)} %copy.11), calls=%async_computation | async-start | bytes 1048576 | tf_op jit(solution)/shard_map/all_to_all | solution.py:43
where the time goes:
time: 76.6 us; the launch traced here: 75.5 us
  blocking collectives  51.5 us (67%)
  starting transfers between devices  7.28 us (10%)
  other arithmetic  6.75 us (9%)
  local copies, waits for them, and re-layouts  5.31 us (7%)
  between operations  2.68 us (3%)
  matrix products  1.91 us (2%)
    psum x1, blocking collectives, per_device(): norm_total = lax.psum(local_square, ('section', 'replica'))  38 us
    unnamed x1, blocking collectives  13.5 us
    all_to_all x1, starting transfers between devices, per_device(): lax.all_to_all(column_parts, 'replica', split_axis=2, concat_axis=0, tile...  7.28 us
    reshape x1, other arithmetic, per_device(): picked = accumulated.reshape(block_total, BLK, width)[slot_ids]  3.04 us
    gather x1, local copies, waits for them, and re-layouts, per_device(): picked = accumulated.reshape(block_total, BLK, width)[slot_ids]  2.74 us
    dot_general x1, matrix products, deposit(): jnp.einsum('kb,kxc->bxc', one_hot, packed, preferred_element_type=jnp.flo...  1.91 us
    sub x1, other arithmetic, per_device(): new_residual = accumulated - sent  1.67 us
  transfers between devices with their start and end apart: 1, of which 0 were waited for; matrix products, arithmetic and copies ran while one was open for 3% of the time, Pallas kernels for 0%

commit v1 on v0

v1 whole, which is shorter than its diff:
```python
import functools

import jax
import jax.numpy as jnp
from jax import lax
from jax.experimental import pallas as pl
from jax.experimental.pallas import tpu as pltpu
from jax.sharding import PartitionSpec as P

BLK = 8
CHUNKS = 4
LANES = 128
MESH = pl.DeviceIdType.MESH

scale_level = 1.0
epsilon = 1e-06


def kernel(
    sections,
    replicas,
    ids_ref,
    counts_ref,
    gradient_ref,
    residual_ref,
    update_ref,
    grad_buf,
    acc_buf,
    packed,
    received,
    target_row,
    targets,
    square_row,
    squares,
    load_sems,
    send_sems,
    recv_sems,
    tsend_sems,
    trecv_sems,
    norm_send,
    norm_recv,
):
    row_count, width = gradient_ref.shape
    block_total = row_count // BLK
    slot_count = ids_ref.shape[1]
    slot_rows = slot_count * BLK
    col_count = width // replicas
    section = lax.axis_index("section")
    replica = lax.axis_index("replica")
    total = sections * replicas
    me = section * replicas + replica

    step = row_count // CHUNKS
    loads = []
    for c in range(CHUNKS):
        rows = pl.ds(c * step, step)
        blocks = pl.ds(c * step // BLK, step // BLK)
        one = pltpu.make_async_copy(gradient_ref.at[rows], grad_buf.at[rows], load_sems.at[0, c])
        two = pltpu.make_async_copy(residual_ref.at[blocks], acc_buf.at[blocks], load_sems.at[1, c])
        one.start()
        two.start()
        loads.append((one, two))

    barrier = pltpu.get_barrier_semaphore()

    def greet(k, carry):
        there = lax.rem(me + k, total)
        pl.semaphore_signal(
            barrier,
            inc=1,
            device_id={"section": there // replicas, "replica": lax.rem(there, replicas)},
            device_id_type=MESH,
        )
        return carry

    lax.fori_loop(1, total, greet, 0)

    lane = lax.broadcasted_iota(jnp.int32, (1, LANES), 1)
    row = jnp.full((1, LANES), -1, jnp.int32)
    for s in range(slot_count):
        base = jnp.where(s < counts_ref[0, 0], ids_ref[0, s] * BLK, -2 * row_count)
        row = jnp.where(lane // BLK == s, base + lane % BLK, row)
    target_row[...] = row

    for c in range(CHUNKS):
        for copy in loads[c]:
            copy.wait()
        rows = pl.ds(c * step, step)
        blocks = pl.ds(c * step // BLK, step // BLK)
        value = grad_buf[rows].astype(jnp.float32).reshape(step // BLK, BLK, width)
        acc_buf[blocks] = acc_buf[blocks] + value

    for s in range(0, slot_count, 2):
        pair = jnp.concatenate([acc_buf[ids_ref[0, s]], acc_buf[ids_ref[0, s + 1]]], axis=0)
        pair = pair.astype(jnp.bfloat16)
        for p in range(replicas):
            packed[p, pl.ds(s * BLK, 2 * BLK), :] = pair[:, p * col_count : (p + 1) * col_count]

    pl.semaphore_wait(barrier, total - 1)

    copies = []
    for k in range(1, replicas):
        peer = lax.rem(replica + k, replicas)
        tcopy = pltpu.make_async_remote_copy(
            src_ref=target_row,
            dst_ref=targets.at[k - 1],
            send_sem=tsend_sems.at[k - 1],
            recv_sem=trecv_sems.at[k - 1],
            device_id={"replica": peer},
            device_id_type=MESH,
        )
        copy = pltpu.make_async_remote_copy(
            src_ref=packed.at[peer],
            dst_ref=received.at[k - 1],
            send_sem=send_sems.at[k - 1],
            recv_sem=recv_sems.at[k - 1],
            device_id={"replica": peer},
            device_id_type=MESH,
        )
        tcopy.start()
        copy.start()
        copies.append((tcopy, copy))

    row_iota = lax.broadcasted_iota(jnp.int32, (row_count, slot_rows), 0)

    def place(wanted, block):
        hot = jnp.where(row_iota == wanted, 1.0, 0.0).astype(jnp.bfloat16)
        return jnp.dot(hot, block, preferred_element_type=jnp.float32)

    summed = place(target_row[:, :slot_rows], packed[replica])
    for k in range(1, replicas):
        tcopy, copy = copies[k - 1]
        tcopy.wait_recv()
        copy.wait_recv()
        summed = summed + place(targets[k - 1][:, :slot_rows], received[k - 1])

    lanes = jnp.sum(summed * summed, axis=0, keepdims=True)
    part = lanes[:, :LANES]
    for j in range(1, col_count // LANES):
        part = part + lanes[:, j * LANES : (j + 1) * LANES]
    square_row[...] = part

    def norm_copy(k):
        there = lax.rem(me + k, total)
        return pltpu.make_async_remote_copy(
            src_ref=square_row,
            dst_ref=squares.at[k - 1],
            send_sem=norm_send,
            recv_sem=norm_recv,
            device_id={"section": there // replicas, "replica": lax.rem(there, replicas)},
            device_id_type=MESH,
        )

    def tell(k, carry):
        norm_copy(k).start()
        return carry

    lax.fori_loop(1, total, tell, 0)
    for tcopy, copy in copies:
        tcopy.wait_send()
        copy.wait_send()
    pltpu.make_async_copy(squares, squares, norm_recv).wait()
    pltpu.make_async_copy(squares, squares, norm_send).wait()
    norm_total = jnp.sum(part + jnp.sum(squares[...], axis=0), axis=1, keepdims=True)
    element_count = sections * row_count * width
    root_mean = jnp.sqrt(norm_total / element_count + epsilon)
    clip_factor = scale_level / root_mean
    update_ref[...] = (summed * clip_factor).astype(jnp.bfloat16)


def per_device(sections, replicas, gradient, residual, block_ids, block_counts):
    row_count, width = gradient.shape
    block_total = row_count // BLK
    slot_count = block_ids.shape[1]
    col_count = width // replicas
    total = sections * replicas
    slot_rows = slot_count * BLK
    update = pl.pallas_call(
        functools.partial(kernel, sections, replicas),
        out_shape=jax.ShapeDtypeStruct((row_count, col_count), jnp.bfloat16),
        in_specs=[
            pl.BlockSpec(memory_space=pltpu.SMEM),
            pl.BlockSpec(memory_space=pltpu.SMEM),
            pl.BlockSpec(memory_space=pl.ANY),
            pl.BlockSpec(memory_space=pl.ANY),
        ],
        out_specs=pl.BlockSpec(memory_space=pltpu.VMEM),
        scratch_shapes=[
            pltpu.VMEM((row_count, width), jnp.bfloat16),
            pltpu.VMEM((block_total, BLK, width), jnp.float32),
            pltpu.VMEM((replicas, slot_rows, col_count), jnp.bfloat16),
            pltpu.VMEM((replicas - 1, slot_rows, col_count), jnp.bfloat16),
            pltpu.VMEM((1, LANES), jnp.int32),
            pltpu.VMEM((replicas - 1, 1, LANES), jnp.int32),
            pltpu.VMEM((1, LANES), jnp.float32),
            pltpu.VMEM((total - 1, 1, LANES), jnp.float32),
            pltpu.SemaphoreType.DMA((2, CHUNKS)),
            pltpu.SemaphoreType.DMA((replicas - 1,)),
            pltpu.SemaphoreType.DMA((replicas - 1,)),
            pltpu.SemaphoreType.DMA((replicas - 1,)),
            pltpu.SemaphoreType.DMA((replicas - 1,)),
            pltpu.SemaphoreType.DMA,
            pltpu.SemaphoreType.DMA,
        ],
        compiler_params=pltpu.CompilerParams(collective_id=0, has_side_effects=True),
    )(block_ids, block_counts, gradient, residual.reshape(block_total, BLK, width))

    accumulated = gradient.astype(jnp.float32) + residual
    live_slot = jnp.arange(slot_count, dtype=jnp.int32) < block_counts[0, 0]
    owner = jnp.arange(row_count, dtype=jnp.int32) // BLK
    row_chosen = jnp.any((owner[:, None] == block_ids) & live_slot[None, :], axis=1, keepdims=True)
    sent = jnp.where(
        row_chosen, accumulated.astype(jnp.bfloat16).astype(jnp.float32), jnp.float32(0.0)
    )
    return (accumulated - sent, update)


def solution(mesh):
    spec = P("section", "replica")
    sizes = (mesh.shape["section"], mesh.shape["replica"])
    return jax.shard_map(
        functools.partial(per_device, *sizes),
        mesh=mesh,
        in_specs=(spec,) * 4,
        out_specs=(spec, spec),
        check_vma=False,
    )
```

time: 76.6 us -> 32.6 us (0.43); the launches traced: 75.5 us -> 32.5 us
  blocking collectives: 51.5 us -> 0 us
  Pallas kernels: 0 us -> 27.8 us
  starting transfers between devices: 7.28 us -> 0 us
  local copies, waits for them, and re-layouts: 5.31 us -> 0.67 us
  other arithmetic: 6.75 us -> 2.54 us
  matrix products: 1.91 us -> 0 us
  between operations: 2.68 us -> 1.49 us
    psum x1 -> x0, blocking collectives: 38 us -> none  [per_device(): norm_total = lax.psum(local_square, ('section', 'replica'))]
    pallas_call x0 -> x1, Pallas kernels: none -> 27.8 us  [per_device(): pl.pallas_call(functools.partial(kernel, sections, replicas), out_shape=j...]
    unnamed x1 -> x0, blocking collectives: 13.5 us -> none
    all_to_all x1 -> x0, starting transfers between devices: 7.28 us -> none  [per_device(): lax.all_to_all(column_parts, 'replica', split_axis=2, concat_axis=0, tile...]
    reshape x1 -> x0, other arithmetic: 3.04 us -> none  [per_device(): picked = accumulated.reshape(block_total, BLK, width)[slot_ids]]
    gather x1 -> x0, local copies, waits for them, and re-layouts: 2.74 us -> none  [per_device(): picked = accumulated.reshape(block_total, BLK, width)[slot_ids]]
    dot_general x1 -> x0, matrix products: 1.91 us -> none  [deposit(): jnp.einsum('kb,kxc->bxc', one_hot, packed, preferred_element_type=jnp.flo...]
    convert_element_type x2 -> x0, local copies, waits for them, and re-layouts: 1.7 us -> none  [the longest x1 0.97 us: per_device(): jnp.where(live_slot[:, None, None], picked, jnp.float32(0.0))]
  transfers between devices with their start and end apart: 1 -> 0, of which waited for: 0 -> 0; matrix products, arithmetic and copies ran while one was open for 3% -> 0% of each run, Pallas kernels for 0% -> 0%
where the time goes in v1:
time: 32.6 us; the launch traced here: 32.5 us
  Pallas kernels  27.8 us (85%)
  other arithmetic  2.54 us (8%)
  between operations  1.49 us (5%)
  local copies, waits for them, and re-layouts  0.67 us (2%)
    pallas_call x1, Pallas kernels, per_device(): pl.pallas_call(functools.partial(kernel, sections, replicas), out_shape=j...  27.8 us
    sub x1, other arithmetic, per_device(): return (accumulated - sent, update)  1.67 us
    reduce_or x1, other arithmetic, per_device(): jnp.any((owner[:, None] == block_ids) & live_slot[None, :], axis=1, keepd...  0.86 us
    unnamed x7, local copies, waits for them, and re-layouts  0.67 us

profile of v1, /device:TPU:0, one launch (start us, length us, event | category | flops | bytes accessed | tf_op | source)
XLA Modules:
  0.0 32.5 jit_solution(16381232911688936180)
XLA Ops:
  0.6 0.0 copy-start
  0.6 0.0 copy-start.1
  1.5 0.9 %and_reduce_fusion = pred[128]{0:T(512)(128)(4,1)S(1)} fusion(s32[128]{0:T(128)S(1)} %and_select_fusion, s32[8]{0:T(128)} %bitcast.5, pred[8]{0:T(512)(128)(4,1)S(1)} %iota_compare_fusion), kind=kLoop, calls=%fused_computation.3 | loop fusion | flops 2944 | bytes 680 | tf_op jit(solution)/shard_map/reduce_or | solution.py:211
  2.3 27.8 %shard_map.59 = bf16[128,512]{1,0:T(8,128)(2,1)} custom-call(s32[1,8]{1,0:T(1,128)} %ids_ref.1, s32[1,1]{1,0:T(1,128)} %copy.7.counts_ref, bf16[128,4096]{1,0:T(8,128)(2,1)} %gradient_ref.1, f32[16,8,4096]{2,1,0:T(8,128)} %bitcast.4), custom_call_target="tpu_custom_call" | custom-call | tf_op jit(solution)/shard_map/pallas_call | solution.py:178
  30.1 0.0 copy-done
  30.1 0.0 copy-done.1
  30.1 0.0 copy-start.2
  30.1 1.7 %select_subtract_fusion = f32[128,4096]{1,0:T(8,128)} fusion(f32[128,4096]{1,0:T(8,128)S(1)} %copy-done, bf16[128,4096]{1,0:T(8,128)(2,1)S(1)} %copy-done.1, pred[128]{0:T(512)(128)(4,1)S(1)} %and_reduce_fusion), kind=kLoop, calls=%fused_computation | loop fusion | flops 3145728 | bytes 5243008 | tf_op jit(solution)/shard_map/sub | solution.py:215
  31.8 0.0 copy-done.2
  31.8 0.7 %copy.8 = bf16[128,512]{1,0:T(8,128)(2,1)} copy(bf16[128,512]{1,0:T(8,128)(2,1)S(1)} %copy-done.2) | data formatting | bytes 262144
  (2 shorter events, 0.0 us)
Async XLA Ops:
  0.6 29.5 %copy-start = (f32[128,4096]{1,0:T(8,128)S(1)}, f32[128,4096]{1,0:T(8,128)}, u32[]{:S(2)}) copy-start(f32[128,4096]{1,0:T(8,128)} %param.5) | copy-start | bytes 6291460
  0.6 29.5 %copy-start.1 = (bf16[128,4096]{1,0:T(8,128)(2,1)S(1)}, bf16[128,4096]{1,0:T(8,128)(2,1)}, u32[]{:S(2)}) copy-start(bf16[128,4096]{1,0:T(8,128)(2,1)} %gradient_ref.1) | copy-start | bytes 3145732
  30.1 1.7 %copy-start.2 = (bf16[128,512]{1,0:T(8,128)(2,1)S(1)}, bf16[128,512]{1,0:T(8,128)(2,1)}, u32[]{:S(2)}) copy-start(bf16[128,512]{1,0:T(8,128)(2,1)} %shard_map.59) | copy-start | bytes 393220

commit v2 on v1

--- a/solution.py
+++ b/solution.py
@@ -24,6 +24,7 @@
     gradient_ref,
     residual_ref,
     update_ref,
+    left_ref,
     grad_buf,
     acc_buf,
     packed,
@@ -48,7 +49,15 @@
     section = lax.axis_index("section")
     replica = lax.axis_index("replica")
     total = sections * replicas
-    me = section * replicas + replica
+
+    def ahead(here, extent):
+        return [here] + [
+            jnp.where(here + k >= extent, here + k - extent, here + k) for k in range(1, extent)
+        ]
+
+    section_at = ahead(section, sections)
+    replica_at = ahead(replica, replicas)
+    others = [(i, j) for i in range(sections) for j in range(replicas) if i + j > 0]
 
     step = row_count // CHUNKS
     loads = []
@@ -63,17 +72,13 @@
 
     barrier = pltpu.get_barrier_semaphore()
 
-    def greet(k, carry):
-        there = lax.rem(me + k, total)
+    for i, j in others:
         pl.semaphore_signal(
             barrier,
             inc=1,
-            device_id={"section": there // replicas, "replica": lax.rem(there, replicas)},
+            device_id={"section": section_at[i], "replica": replica_at[j]},
             device_id_type=MESH,
         )
-        return carry
-
-    lax.fori_loop(1, total, greet, 0)
 
     lane = lax.broadcasted_iota(jnp.int32, (1, LANES), 1)
     row = jnp.full((1, LANES), -1, jnp.int32)
@@ -100,7 +105,7 @@
 
     copies = []
     for k in range(1, replicas):
-        peer = lax.rem(replica + k, replicas)
+        peer = replica_at[k]
         tcopy = pltpu.make_async_remote_copy(
             src_ref=target_row,
             dst_ref=targets.at[k - 1],
@@ -121,6 +126,16 @@
         copy.start()
         copies.append((tcopy, copy))
 
+    for c in range(CHUNKS):
+        for b in range(c * step // BLK, (c + 1) * step // BLK):
+            chosen = jnp.int32(0)
+            for s in range(slot_count):
+                hit = (ids_ref[0, s] == b) & (s < counts_ref[0, 0])
+                chosen = jnp.where(hit, 1, chosen)
+            value = acc_buf[b]
+            rounded = value.astype(jnp.bfloat16).astype(jnp.float32)
+            left_ref[b] = value - jnp.where(chosen > 0, rounded, 0.0)
+
     row_iota = lax.broadcasted_iota(jnp.int32, (row_count, slot_rows), 0)
 
     def place(wanted, block):
@@ -140,22 +155,15 @@
         part = part + lanes[:, j * LANES : (j + 1) * LANES]
     square_row[...] = part
 
-    def norm_copy(k):
-        there = lax.rem(me + k, total)
-        return pltpu.make_async_remote_copy(
+    for slot, (i, j) in enumerate(others):
+        pltpu.make_async_remote_copy(
             src_ref=square_row,
-            dst_ref=squares.at[k - 1],
+            dst_ref=squares.at[slot],
             send_sem=norm_send,
             recv_sem=norm_recv,
-            device_id={"section": there // replicas, "replica": lax.rem(there, replicas)},
-            device_id_type=MESH,
-        )
-
-    def tell(k, carry):
-        norm_copy(k).start()
-        return carry
-
-    lax.fori_loop(1, total, tell, 0)
+            device_id={"section": section_at[i], "replica": replica_at[j]},
+            device_id_type=MESH,
+        ).start()
     for tcopy, copy in copies:
         tcopy.wait_send()
         copy.wait_send()
@@ -175,16 +183,22 @@
     col_count = width // replicas
     total = sections * replicas
     slot_rows = slot_count * BLK
-    update = pl.pallas_call(
+    update, left = pl.pallas_call(
         functools.partial(kernel, sections, replicas),
-        out_shape=jax.ShapeDtypeStruct((row_count, col_count), jnp.bfloat16),
+        out_shape=(
+            pltpu.VMEM((row_count, col_count), jnp.bfloat16),
+            pltpu.VMEM((block_total, BLK, width), jnp.float32),
+        ),
         in_specs=[
             pl.BlockSpec(memory_space=pltpu.SMEM),
             pl.BlockSpec(memory_space=pltpu.SMEM),
             pl.BlockSpec(memory_space=pl.ANY),
             pl.BlockSpec(memory_space=pl.ANY),
         ],
-        out_specs=pl.BlockSpec(memory_space=pltpu.VMEM),
+        out_specs=(
+            pl.BlockSpec(memory_space=pltpu.VMEM),
+            pl.BlockSpec(memory_space=pltpu.VMEM),
+        ),
         scratch_shapes=[
             pltpu.VMEM((row_count, width), jnp.bfloat16),
             pltpu.VMEM((block_total, BLK, width), jnp.float32),
@@ -205,14 +219,7 @@
         compiler_params=pltpu.CompilerParams(collective_id=0, has_side_effects=True),
     )(block_ids, block_counts, gradient, residual.reshape(block_total, BLK, width))
 
-    accumulated = gradient.astype(jnp.float32) + residual
-    live_slot = jnp.arange(slot_count, dtype=jnp.int32) < block_counts[0, 0]
-    owner = jnp.arange(row_count, dtype=jnp.int32) // BLK
-    row_chosen = jnp.any((owner[:, None] == block_ids) & live_slot[None, :], axis=1, keepdims=True)
-    sent = jnp.where(
-        row_chosen, accumulated.astype(jnp.bfloat16).astype(jnp.float32), jnp.float32(0.0)
-    )
-    return (accumulated - sent, update)
+    return (left.reshape(row_count, width), update)
 
 
 def solution(mesh):

time: 32.6 us -> 29.9 us (0.917)
  other arithmetic: 2.54 us -> 0 us
  local copies, waits for them, and re-layouts: 0.67 us -> 1.98 us
  Pallas kernels: 27.8 us -> 26.5 us
    sub x1 -> x0, other arithmetic: 1.67 us -> none  [per_device(): return (accumulated - sent, update)]
    unnamed x7 -> x2, local copies, waits for them, and re-layouts: 0.67 us -> 1.98 us
    pallas_call x1, Pallas kernels: 27.8 us -> 26.5 us  [per_device(): pl.pallas_call(functools.partial(kernel, sections, replicas), out_shape=(...]
    reduce_or x1 -> x0, other arithmetic: 0.86 us -> none  [per_device(): jnp.any((owner[:, None] == block_ids) & live_slot[None, :], axis=1, keepd...]
where the time goes in v2:
time: 29.9 us; the launch traced here: 29.7 us
  Pallas kernels  26.5 us (89%)
  local copies, waits for them, and re-layouts  1.98 us (7%)
  between operations  1.29 us (4%)
    pallas_call x1, Pallas kernels, per_device(): pl.pallas_call(functools.partial(kernel, sections, replicas), out_shape=(...  26.5 us
    unnamed x2, local copies, waits for them, and re-layouts  1.98 us

profile of v2, /device:TPU:0, one launch (start us, length us, event | category | flops | bytes accessed | tf_op | source)
XLA Modules:
  0.0 29.7 jit_solution(10568887575242338368)
XLA Ops:
  1.3 26.5 %shard_map.59 = (bf16[128,512]{1,0:T(8,128)(2,1)S(1)}, f32[16,8,4096]{2,1,0:T(8,128)S(1)}) custom-call(s32[1,8]{1,0:T(1,128)} %ids_ref.1, s32[1,1]{1,0:T(1,128)S(6)} %copy.10.counts_ref, bf16[128,4096]{1,0:T(8,128)(2,1)} %gradient_ref.1, f32[16,8,4096]{2,1,0:T(8,128)} %bitcast.3), custom_call_target="tpu_custom_call" | custom-call | tf_op jit(solution)/shard_map/pallas_call | solution.py:186
  27.8 1.3 %copy.8 = f32[128,4096]{1,0:T(8,128)} copy(f32[128,4096]{1,0:T(8,128)S(1)} %bitcast.2) | data formatting | bytes 4194304
  29.1 0.7 %copy.9 = bf16[128,512]{1,0:T(8,128)(2,1)} copy(bf16[128,512]{1,0:T(8,128)(2,1)S(1)} %get-tuple-element.7) | data formatting | bytes 262144

commit v3 on v2

--- a/solution.py
+++ b/solution.py
@@ -34,10 +34,17 @@
     square_row,
     squares,
     load_sems,
-    send_sems,
-    recv_sems,
-    tsend_sems,
-    trecv_sems,
+    relayed,
+    far_targets,
+    far_data,
+    cross_buf,
+    cross_in,
+    relay_sems,
+    near_row_sems,
+    near_sems,
+    far_row_sems,
+    far_sems,
+    cross_sems,
     norm_send,
     norm_recv,
 ):
@@ -45,6 +52,9 @@
     block_total = row_count // BLK
     slot_count = ids_ref.shape[1]
     slot_rows = slot_count * BLK
+    cap = slot_count // 2
+    cap_rows = cap * BLK
+    half = replicas // 2
     col_count = width // replicas
     section = lax.axis_index("section")
     replica = lax.axis_index("replica")
@@ -96,35 +106,48 @@
         acc_buf[blocks] = acc_buf[blocks] + value
 
     for s in range(0, slot_count, 2):
-        pair = jnp.concatenate([acc_buf[ids_ref[0, s]], acc_buf[ids_ref[0, s + 1]]], axis=0)
-        pair = pair.astype(jnp.bfloat16)
+        pair = [acc_buf[ids_ref[0, s + i]] for i in range(2)]
+        if s >= cap:
+            pair = [jnp.where(s + i < counts_ref[0, 0], pair[i], 0.0) for i in range(2)]
+        pair = jnp.concatenate(pair, axis=0).astype(jnp.bfloat16)
         for p in range(replicas):
             packed[p, pl.ds(s * BLK, 2 * BLK), :] = pair[:, p * col_count : (p + 1) * col_count]
 
     pl.semaphore_wait(barrier, total - 1)
 
-    copies = []
-    for k in range(1, replicas):
-        peer = replica_at[k]
-        tcopy = pltpu.make_async_remote_copy(
-            src_ref=target_row,
-            dst_ref=targets.at[k - 1],
-            send_sem=tsend_sems.at[k - 1],
-            recv_sem=trecv_sems.at[k - 1],
+    side = replica // half * half
+    other_side = half - side
+    place_in_side = replica - side
+    inner = [
+        jnp.where(place_in_side + k >= half, place_in_side + k - half, place_in_side + k)
+        for k in range(half)
+    ]
+
+    def send(src, dst, sems, slot, peer):
+        copy = pltpu.make_async_remote_copy(
+            src_ref=src,
+            dst_ref=dst,
+            send_sem=sems.at[0, slot],
+            recv_sem=sems.at[1, slot],
             device_id={"replica": peer},
             device_id_type=MESH,
         )
-        copy = pltpu.make_async_remote_copy(
-            src_ref=packed.at[peer],
-            dst_ref=received.at[k - 1],
-            send_sem=send_sems.at[k - 1],
-            recv_sem=recv_sems.at[k - 1],
-            device_id={"replica": peer},
-            device_id_type=MESH,
-        )
-        tcopy.start()
         copy.start()
-        copies.append((tcopy, copy))
+        return copy
+
+    relay_in, near_rows, near, far_rows, far = {}, {}, {}, {}, {}
+    for k in range(half - 1, 0, -1):
+        peer = side + inner[k]
+        source = packed.at[other_side + inner[k], pl.ds(cap_rows, slot_rows - cap_rows)]
+        relay_in[k] = send(source, relayed.at[k - 1], relay_sems, k - 1, peer)
+    for k in range(half - 1, -1, -1):
+        peer = other_side + inner[k]
+        far_rows[k] = send(target_row, far_targets.at[k], far_row_sems, k, peer)
+        far[k] = send(packed.at[peer, pl.ds(0, cap_rows)], far_data.at[k], far_sems, k, peer)
+    for k in range(half - 1, 0, -1):
+        peer = side + inner[k]
+        near_rows[k] = send(target_row, targets.at[k - 1], near_row_sems, k - 1, peer)
+        near[k] = send(packed.at[peer], received.at[k - 1], near_sems, k - 1, peer)
 
     for c in range(CHUNKS):
         for b in range(c * step // BLK, (c + 1) * step // BLK):
@@ -136,18 +159,33 @@
             rounded = value.astype(jnp.bfloat16).astype(jnp.float32)
             left_ref[b] = value - jnp.where(chosen > 0, rounded, 0.0)
 
-    row_iota = lax.broadcasted_iota(jnp.int32, (row_count, slot_rows), 0)
 
     def place(wanted, block):
+        row_iota = lax.broadcasted_iota(jnp.int32, (row_count, wanted.shape[1]), 0)
         hot = jnp.where(row_iota == wanted, 1.0, 0.0).astype(jnp.bfloat16)
         return jnp.dot(hot, block, preferred_element_type=jnp.float32)
 
+    crossing = packed[other_side + place_in_side, cap_rows:, :].astype(jnp.float32)
+    for k in range(1, half):
+        relay_in[k].wait_recv()
+        crossing = crossing + relayed[k - 1].astype(jnp.float32)
+    cross_buf[...] = crossing.astype(jnp.bfloat16)
+    cross = send(cross_buf, cross_in, cross_sems, 0, other_side + place_in_side)
+
     summed = place(target_row[:, :slot_rows], packed[replica])
-    for k in range(1, replicas):
-        tcopy, copy = copies[k - 1]
-        tcopy.wait_recv()
-        copy.wait_recv()
+    for k in range(1, half):
+        near_rows[k].wait_recv()
+        near[k].wait_recv()
         summed = summed + place(targets[k - 1][:, :slot_rows], received[k - 1])
+    wanted = jnp.full((1, slot_rows), -1, jnp.int32)
+    for k in range(half):
+        far_rows[k].wait_recv()
+        far[k].wait_recv()
+        theirs = far_targets[k][:, :slot_rows]
+        wanted = jnp.maximum(wanted, theirs)
+        summed = summed + place(theirs[:, :cap_rows], far_data[k])
+    cross.wait_recv()
+    summed = summed + place(wanted[:, cap_rows:], cross_in[...])
 
     lanes = jnp.sum(summed * summed, axis=0, keepdims=True)
     part = lanes[:, :LANES]
@@ -164,9 +202,9 @@
             device_id={"section": section_at[i], "replica": replica_at[j]},
             device_id_type=MESH,
         ).start()
-    for tcopy, copy in copies:
-        tcopy.wait_send()
-        copy.wait_send()
+    for group in (relay_in, near_rows, near, far_rows, far, {0: cross}):
+        for copy in group.values():
+            copy.wait_send()
     pltpu.make_async_copy(squares, squares, norm_recv).wait()
     pltpu.make_async_copy(squares, squares, norm_send).wait()
     norm_total = jnp.sum(part + jnp.sum(squares[...], axis=0), axis=1, keepdims=True)
@@ -183,6 +221,8 @@
     col_count = width // replicas
     total = sections * replicas
     slot_rows = slot_count * BLK
+    over_rows = slot_rows - slot_count // 2 * BLK
+    half = replicas // 2
     update, left = pl.pallas_call(
         functools.partial(kernel, sections, replicas),
         out_shape=(
@@ -203,16 +243,23 @@
             pltpu.VMEM((row_count, width), jnp.bfloat16),
             pltpu.VMEM((block_total, BLK, width), jnp.float32),
             pltpu.VMEM((replicas, slot_rows, col_count), jnp.bfloat16),
-            pltpu.VMEM((replicas - 1, slot_rows, col_count), jnp.bfloat16),
+            pltpu.VMEM((half - 1, slot_rows, col_count), jnp.bfloat16),
             pltpu.VMEM((1, LANES), jnp.int32),
-            pltpu.VMEM((replicas - 1, 1, LANES), jnp.int32),
+            pltpu.VMEM((half - 1, 1, LANES), jnp.int32),
             pltpu.VMEM((1, LANES), jnp.float32),
             pltpu.VMEM((total - 1, 1, LANES), jnp.float32),
             pltpu.SemaphoreType.DMA((2, CHUNKS)),
-            pltpu.SemaphoreType.DMA((replicas - 1,)),
-            pltpu.SemaphoreType.DMA((replicas - 1,)),
-            pltpu.SemaphoreType.DMA((replicas - 1,)),
-            pltpu.SemaphoreType.DMA((replicas - 1,)),
+            pltpu.VMEM((half - 1, over_rows, col_count), jnp.bfloat16),
+            pltpu.VMEM((half, 1, LANES), jnp.int32),
+            pltpu.VMEM((half, slot_rows - over_rows, col_count), jnp.bfloat16),
+            pltpu.VMEM((over_rows, col_count), jnp.bfloat16),
+            pltpu.VMEM((over_rows, col_count), jnp.bfloat16),
+            pltpu.SemaphoreType.DMA((2, half - 1)),
+            pltpu.SemaphoreType.DMA((2, half - 1)),
+            pltpu.SemaphoreType.DMA((2, half - 1)),
+            pltpu.SemaphoreType.DMA((2, half)),
+            pltpu.SemaphoreType.DMA((2, half)),
+            pltpu.SemaphoreType.DMA((2, 1)),
             pltpu.SemaphoreType.DMA,
             pltpu.SemaphoreType.DMA,
         ],

time: 29.9 us -> 25.4 us (0.85)
  Pallas kernels: 26.5 us -> 22 us
    pallas_call x1, Pallas kernels: 26.5 us -> 22 us  [per_device(): pl.pallas_call(functools.partial(kernel, sections, replicas), out_shape=(...]
where the time goes in v3:
time: 25.4 us; the launch traced here: 25.3 us
  Pallas kernels  22 us (87%)
  local copies, waits for them, and re-layouts  1.98 us (8%)
  between operations  1.29 us (5%)
    pallas_call x1, Pallas kernels, per_device(): pl.pallas_call(functools.partial(kernel, sections, replicas), out_shape=(...  22 us
    unnamed x2, local copies, waits for them, and re-layouts  1.98 us

profile of v3, /device:TPU:0, one launch (start us, length us, event | category | flops | bytes accessed | tf_op | source)
XLA Modules:
  0.0 25.3 jit_solution(12543127192535674609)
XLA Ops:
  1.3 22.0 %shard_map.59 = (bf16[128,512]{1,0:T(8,128)(2,1)S(1)}, f32[16,8,4096]{2,1,0:T(8,128)S(1)}) custom-call(s32[1,8]{1,0:T(1,128)} %ids_ref.1, s32[1,1]{1,0:T(1,128)S(6)} %copy.10.counts_ref, bf16[128,4096]{1,0:T(8,128)(2,1)} %gradient_ref.1, f32[16,8,4096]{2,1,0:T(8,128)} %bitcast.3), custom_call_target="tpu_custom_call" | custom-call | tf_op jit(solution)/shard_map/pallas_call | solution.py:226
  23.3 1.3 %copy.8 = f32[128,4096]{1,0:T(8,128)} copy(f32[128,4096]{1,0:T(8,128)S(1)} %bitcast.2) | data formatting | bytes 4194304
  24.6 0.7 %copy.9 = bf16[128,512]{1,0:T(8,128)(2,1)} copy(bf16[128,512]{1,0:T(8,128)(2,1)S(1)} %get-tuple-element.7) | data formatting | bytes 262144

commit v4 on v3

--- a/solution.py
+++ b/solution.py
@@ -19,8 +19,8 @@
 def kernel(
     sections,
     replicas,
-    ids_ref,
-    counts_ref,
+    ids_hbm,
+    counts_hbm,
     gradient_ref,
     residual_ref,
     update_ref,
@@ -34,6 +34,9 @@
     square_row,
     squares,
     load_sems,
+    ids_ref,
+    counts_ref,
+    list_sems,
     relayed,
     far_targets,
     far_data,
@@ -50,7 +53,7 @@
 ):
     row_count, width = gradient_ref.shape
     block_total = row_count // BLK
-    slot_count = ids_ref.shape[1]
+    slot_count = ids_hbm.shape[1]
     slot_rows = slot_count * BLK
     cap = slot_count // 2
     cap_rows = cap * BLK
@@ -68,6 +71,13 @@
     section_at = ahead(section, sections)
     replica_at = ahead(replica, replicas)
     others = [(i, j) for i in range(sections) for j in range(replicas) if i + j > 0]
+
+    lists = [
+        pltpu.make_async_copy(ids_hbm, ids_ref, list_sems.at[0]),
+        pltpu.make_async_copy(counts_hbm, counts_ref, list_sems.at[1]),
+    ]
+    for copy in lists:
+        copy.start()
 
     step = row_count // CHUNKS
     loads = []
@@ -90,6 +100,8 @@
             device_id_type=MESH,
         )
 
+    for copy in lists:
+        copy.wait()
     lane = lax.broadcasted_iota(jnp.int32, (1, LANES), 1)
     row = jnp.full((1, LANES), -1, jnp.int32)
     for s in range(slot_count):
@@ -230,8 +242,8 @@
             pltpu.VMEM((block_total, BLK, width), jnp.float32),
         ),
         in_specs=[
-            pl.BlockSpec(memory_space=pltpu.SMEM),
-            pl.BlockSpec(memory_space=pltpu.SMEM),
+            pl.BlockSpec(memory_space=pl.ANY),
+            pl.BlockSpec(memory_space=pl.ANY),
             pl.BlockSpec(memory_space=pl.ANY),
             pl.BlockSpec(memory_space=pl.ANY),
         ],
@@ -249,6 +261,9 @@
             pltpu.VMEM((1, LANES), jnp.float32),
             pltpu.VMEM((total - 1, 1, LANES), jnp.float32),
             pltpu.SemaphoreType.DMA((2, CHUNKS)),
+            pltpu.SMEM(block_ids.shape, jnp.int32),
+            pltpu.SMEM(block_counts.shape, jnp.int32),
+            pltpu.SemaphoreType.DMA((2,)),
             pltpu.VMEM((half - 1, over_rows, col_count), jnp.bfloat16),
             pltpu.VMEM((half, 1, LANES), jnp.int32),
             pltpu.VMEM((half, slot_rows - over_rows, col_count), jnp.bfloat16),

time: 25.4 us -> 24.8 us (0.976)
  Pallas kernels: 22 us -> 21.4 us
    pallas_call x1, Pallas kernels: 22 us -> 21.4 us  [per_device(): pl.pallas_call(functools.partial(kernel, sections, replicas), out_shape=(...]
where the time goes in v4:
time: 24.8 us; the launch traced here: 24.6 us
  Pallas kernels  21.4 us (86%)
  local copies, waits for them, and re-layouts  1.98 us (8%)
  between operations  1.29 us (5%)
    pallas_call x1, Pallas kernels, per_device(): pl.pallas_call(functools.partial(kernel, sections, replicas), out_shape=(...  21.4 us
    unnamed x2, local copies, waits for them, and re-layouts  1.98 us

profile of v4, /device:TPU:0, one launch (start us, length us, event | category | flops | bytes accessed | tf_op | source)
XLA Modules:
  0.0 24.6 jit_solution(15493856532713030258)
XLA Ops:
  1.3 21.4 %shard_map.59 = (bf16[128,512]{1,0:T(8,128)(2,1)S(1)}, f32[16,8,4096]{2,1,0:T(8,128)S(1)}) custom-call(s32[1,8]{1,0:T(1,128)} %ids_hbm.1, s32[1,1]{1,0:T(1,128)S(6)} %copy.10.counts_hbm, bf16[128,4096]{1,0:T(8,128)(2,1)} %gradient_ref.1, f32[16,8,4096]{2,1,0:T(8,128)} %bitcast.3), custom_call_target="tpu_custom_call" | custom-call | tf_op jit(solution)/shard_map/pallas_call | solution.py:238
  22.6 1.3 %copy.8 = f32[128,4096]{1,0:T(8,128)} copy(f32[128,4096]{1,0:T(8,128)S(1)} %bitcast.2) | data formatting | bytes 4194304
  24.0 0.7 %copy.9 = bf16[128,512]{1,0:T(8,128)(2,1)} copy(bf16[128,512]{1,0:T(8,128)(2,1)S(1)} %get-tuple-element.7) | data formatting | bytes 262144
